TPU v7x, 32 devices: a whole 2x2x4 slice. The times are simulated.
32 devices in a mesh: dp: 16 (over z, y, x), mp: 2 (over core).
Axes of the slice: x: 2, y: 2, z: 4, core: 2. Of those that a mesh axis runs over, the one named last changes fastest.
Arguments:
- embeddings: float32 [12288, 1024], P('dp', 'mp')
- cluster_id: int32 [12288], P('dp'), may hold values from 0 to 4095, as said below
- centroids: float32 [4096, 1024], P('dp', 'mp'), may hold values from -6 to 6
- cluster_mass: float32 [4096], P('dp'), may hold values from 1 to 16
Outputs:
- max_similarity: float32 [12288], P('dp')
- new_centroids: float32 [4096, 1024], P('dp', 'mp')
Inputs may be any that keep to these rules, and one draw needn't show every extreme that they name: `cluster_id`: cluster k belongs to owner k // 256. Among the 768 rows of one index of dp, at most 96 have clusters of any one owner, and for some owner exactly 96.
All inputs are finite; a program needn't handle non-finite values.
Results may differ from a plain program's by a relative error of at most 0.0011.
Values may be sent and summed in bfloat16 or wider, within the bound.
No kernel may reach another device: no remote copies, remote signals or barrier semaphores. Data moves between devices by JAX's collectives and lax.ppermute only.
A program may use at most 64 MiB of HBM per device.

v0:
```python
import jax
import jax.numpy as jnp
from jax import lax
from jax.sharding import PartitionSpec as P

D = 1024


def shards(embeddings, cluster_id, centroids, cluster_mass):
    owners = lax.axis_size("dp")
    row_count = embeddings.shape[0]
    slot_count = 2 * row_count
    capacity = slot_count // owners
    cluster_count = centroids.shape[0]
    squares = lax.psum(jnp.sum(embeddings * embeddings, axis=1), "mp")
    unit = (embeddings * lax.rsqrt(squares / D + 1e-06)[:, None]).astype(jnp.bfloat16)
    owner = cluster_id // cluster_count
    local = cluster_id - owner * cluster_count
    owner_hot = (owner[:, None] == jnp.arange(owners, dtype=jnp.int32)[None, :]).astype(
        jnp.bfloat16
    )
    row_index = jnp.arange(row_count, dtype=jnp.int32)
    lower = (row_index[:, None] >= row_index[None, :]).astype(jnp.bfloat16)
    running = jnp.dot(lower, owner_hot, preferred_element_type=jnp.float32)
    rank = jnp.sum(running * owner_hot.astype(jnp.float32), axis=1).astype(jnp.int32) - 1
    slot = owner * capacity + rank
    slot_index = jnp.arange(slot_count, dtype=jnp.int32)
    placed = slot_index[:, None] == slot[None, :]
    outgoing = jnp.dot(
        placed.astype(jnp.bfloat16), unit, preferred_element_type=jnp.float32
    ).astype(jnp.bfloat16)
    out_ids = jnp.max(jnp.where(placed, local[None, :] + 1, 0), axis=1) - 1
    incoming, in_ids = (
        lax.all_to_all(outgoing, "dp", split_axis=0, concat_axis=0, tiled=True),
        lax.all_to_all(out_ids, "dp", split_axis=0, concat_axis=0, tiled=True),
    )
    member = (jnp.arange(cluster_count, dtype=jnp.int32)[:, None] == in_ids[None, :]).astype(
        jnp.bfloat16
    )
    sums = jnp.dot(member, incoming, preferred_element_type=jnp.float32)
    counts = jnp.sum(member.astype(jnp.float32), axis=1)
    new_centroids = (cluster_mass[:, None] * centroids + sums) / (cluster_mass + counts)[:, None]
    half = slot_count // lax.axis_size("mp")
    start = lax.axis_index("mp") * half
    contract = (((1,), (1,)), ((), ()))
    gathered = lax.all_gather(incoming, "mp", axis=1, tiled=True)
    queries = lax.dynamic_slice_in_dim(gathered, start, half, 0)
    scores = lax.dot_general(queries, gathered, contract, preferred_element_type=jnp.float32)
    scores = scores / D
    query_ids = lax.dynamic_slice_in_dim(in_ids, start, half, 0)
    query_pos = start + jnp.arange(half, dtype=jnp.int32)
    same = (
        (query_ids[:, None] == in_ids[None, :])
        & (query_ids[:, None] >= 0)
        & (query_pos[:, None] != slot_index[None, :])
    )
    best = jnp.max(jnp.where(same, scores, -1.0), axis=1)
    best_all = lax.all_gather(best, "mp", axis=0, tiled=True)
    returned = lax.all_to_all(best_all, "dp", split_axis=0, concat_axis=0, tiled=True)
    max_similarity = jnp.take(returned, slot)
    return (max_similarity, new_centroids)


def solution(mesh):
    in_specs = (P("dp", "mp"), P("dp"), P("dp", "mp"), P("dp"))
    out_specs = (P("dp"), P("dp", "mp"))
    return jax.shard_map(shards, mesh=mesh, in_specs=in_specs, out_specs=out_specs, check_vma=False)
```

profile of v0, /device:TPU:0, one launch (start us, length us, event | category | flops | bytes accessed | tf_op | source)
XLA Modules:
  0.0 107.2 jit_solution(10581560315133862556)
XLA Ops:
  7.2 0.0 copy-start.1
  7.2 0.0 all-gather.3.cloned.1.call-start
  7.2 0.8 add_select_fusion
  8.0 0.3 fusion.11
  8.4 0.7 compare_select_fusion
  9.1 1.6 %multiply_reduce_fusion = f32[768]{0:T(1024)S(1)} fusion(f32[768,512]{1,0:T(8,128)} %param.4), kind=kLoop, calls=%fused_computation.17 | loop fusion | flops 785664 | bytes 1575936 | tf_op jit(solution)/shard_map/reduce_sum | solution.py:15
  10.7 2.6 %psum.7 = f32[768]{0:T(1024)S(1)} all-reduce(f32[768]{0:T(1024)S(1)} %multiply_reduce_fusion), channel_id=1, replica_groups=mesh['dp'=16,'mp'=2] {'mp'}, use_global_device_ids=true, to_apply=%region_3.4 | all-reduce | flops 768 | bytes 6144 | tf_op jit(solution)/shard_map/psum | solution.py:15
  13.3 0.0 copy-done.1
  13.3 1.5 %fusion.2 = bf16[1536,512]{1,0:T(8,128)(2,1)S(1)} fusion(s32[768]{0:T(1024)S(1)} %get-tuple-element.3, f32[768,512]{1,0:T(8,128)S(1)} %copy-done.1, f32[768]{0:T(1024)S(1)} %add_rsqrt_fusion), kind=kOutput, calls=%fused_computation.7 | convolution fusion | flops 1210712064 | bytes 3151872 | tf_op jit(solution)/shard_map/dot_general | solution.py:29
  14.8 46.0 %all_to_all.33 = bf16[16,96,512]{2,1,0:T(8,128)(2,1)} all-to-all(bf16[16,96,512]{2,1,0:T(8,128)(2,1)S(1)} %bitcast.10), channel_id=1, replica_groups=mesh['dp'=16,'mp'=2] {'dp'}, dimensions={0} | all-to-all | bytes 3145728 | tf_op jit(solution)/shard_map/all_to_all | solution.py:34
  60.8 0.0 copy-start.2
  60.8 0.0 all-gather.3.cloned.1.call-update
  60.8 0.7 select_reduce_fusion.1
  61.5 0.7 sub.23
  62.2 3.9 %all-to-all-start = ((s32[16,96,1]{1,2,0:T(1,128)}), s32[16,96,1]{1,2,0:T(1,128)S(1)}, u32[]{:S(2)}, u32[]{:S(2)}) async-start(s32[16,96,1]{1,2,0:T(1,128)} %bitcast), calls=%async_computation | async-start | bytes 16384 | tf_op jit(solution)/shard_map/all_to_all | solution.py:35
  66.2 7.2 %all-to-all-done = s32[16,96,1]{1,2,0:T(1,128)S(1)} async-done(((s32[16,96,1]{1,2,0:T(1,128)}), s32[16,96,1]{1,2,0:T(1,128)S(1)}, u32[]{:S(2)}, u32[]{:S(2)}) %all-to-all-start) | async-done | bytes 6176 | tf_op jit(solution)/shard_map/all_to_all | solution.py:35
  73.4 0.5 broadcast.71
  73.9 0.7 reduce.7
  74.6 0.1 all_to_all.23
  74.6 0.2 convert_reduce_fusion
  74.9 0.0 copy-done.2
  74.9 0.1 broadcast_compare_fusion
  75.0 0.0 all-gather.3.cloned.1.call-done
  75.0 0.0 copy-start
  75.0 0.0 copy-start.3
  75.0 5.8 %select_reduce_fusion = f32[768]{0:T(1024)S(1)} fusion(bf16[1536,1024]{1,0:T(8,128)(2,1)} %all-gather.3.cloned.1.call-done, s32[768]{0:T(1024)S(1)} %iota_add_fusion, s32[1536]{0:T(1024)S(1)} %all_to_all.23, s32[768]{0:T(1024)S(1)} %get-tuple-element.5, pred[768]{0:T(1024)(128)(4,1)S(1)} %get-tuple-element.4, s32[]{:T(128)S(6)} %select_n.28), kind=kOutput, calls=%fused_computation.1 | convolution fusion | flops 2424175872 | bytes 4734724 | tf_op jit(solution)/shard_map/dot_general | solution.py:48
  80.8 1.8 %all-gather = f32[2,1,768]{2,1,0:T(1,128)S(1)} all-gather(f32[1,1,768]{2,1,0:T(1,128)S(1)} %reshape.52), channel_id=1, replica_groups=mesh['dp'=16,'mp'=2] {'mp'}, dimensions={0}, use_global_device_ids=true | all-gather | bytes 9216 | tf_op jit(solution)/shard_map/all_gather | solution.py:58
  82.6 0.7 all_to_all.27
  83.3 3.5 %all-to-all-start.2 = ((f32[16,96,1]{1,2,0:T(1,128)}), f32[16,96,1]{1,2,0:T(1,128)S(1)}, u32[]{:S(2)}, u32[]{:S(2)}) async-start(f32[16,96,1]{1,2,0:T(1,128)} %bitcast.3), calls=%async_computation.2 | async-start | bytes 16384 | tf_op jit(solution)/shard_map/all_to_all | solution.py:59
  86.8 0.0 copy-done
  86.8 0.0 copy-done.3
  86.8 1.4 %fusion.9 = f32[256,512]{1,0:T(8,128)} fusion(bf16[1536,512]{1,0:T(8,128)(2,1)S(1)} %bitcast.9, s32[1536]{0:T(1024)S(1)} %all_to_all.23, f32[256,512]{1,0:T(8,128)S(1)} %copy-done.3, f32[256]{0:T(256)S(1)} %add.65, f32[256]{0:T(256)S(1)} %copy-done.2), kind=kOutput, calls=%fused_computation.19 | convolution fusion | flops 403439616 | bytes 2629632 | tf_op jit(solution)/shard_map/dot_general | solution.py:40
  88.2 5.9 %all-to-all-done.2 = f32[16,96,1]{1,2,0:T(1,128)S(1)} async-done(((f32[16,96,1]{1,2,0:T(1,128)}), f32[16,96,1]{1,2,0:T(1,128)S(1)}, u32[]{:S(2)}, u32[]{:S(2)}) %all-to-all-start.2) | async-done | bytes 6176 | tf_op jit(solution)/shard_map/all_to_all | solution.py:59
  94.1 0.5 broadcast.72
  94.6 0.7 reduce.8
  95.3 0.1 all_to_all.29
  95.3 4.5 %gather_fusion = f32[768]{0:T(1024)S(1)} fusion(f32[1536]{0:T(1024)S(1)} %all_to_all.29, s32[1024]{0:T(1024)S(1)} %pad_clamp_fusion), kind=kCustom, calls=%fused_computation | custom fusion | bytes 9216 | tf_op jit(solution)/shard_map/jit(_take)/gather | solution.py:60
  99.8 0.6 and_select_fusion
  (7 shorter events, 0.1 us)
Async XLA Ops:
  7.2 6.2 %copy-start.1 = (f32[768,512]{1,0:T(8,128)S(1)}, f32[768,512]{1,0:T(8,128)}, u32[]{:S(2)}) copy-start(f32[768,512]{1,0:T(8,128)} %param.4) | copy-start | bytes 4718596
  7.2 67.8 %all-gather.3.cloned.1.call-start = ((), (), s32[]{:S(2)}) async-start(), calls=%async_computation.3 | async-start | bytes 4718592 | tf_op jit(solution)/shard_map/all_gather | solution.py:46
  60.8 14.1 %copy-start.2 = (f32[256]{0:T(256)S(1)}, f32[256]{0:T(256)}, u32[]{:S(2)}) copy-start(f32[256]{0:T(256)} %param.7) | copy-start | bytes 3076
  62.2 11.2 %all-to-all-start = ((s32[16,96,1]{1,2,0:T(1,128)}), s32[16,96,1]{1,2,0:T(1,128)S(1)}, u32[]{:S(2)}, u32[]{:S(2)}) async-start(s32[16,96,1]{1,2,0:T(1,128)} %bitcast), calls=%async_computation | async-start | bytes 16384 | tf_op jit(solution)/shard_map/all_to_all | solution.py:35
  75.0 11.8 %copy-start = (bf16[16,96,512]{2,1,0:T(8,128)(2,1)S(1)}, bf16[16,96,512]{2,1,0:T(8,128)(2,1)}, u32[]{:S(2)}) copy-start(bf16[16,96,512]{2,1,0:T(8,128)(2,1)} %all_to_all.33) | copy-start | bytes 4718596
  75.0 11.8 %copy-start.3 = (f32[256,512]{1,0:T(8,128)S(1)}, f32[256,512]{1,0:T(8,128)}, u32[]{:S(2)}) copy-start(f32[256,512]{1,0:T(8,128)} %param.6) | copy-start | bytes 1572868
  83.3 10.8 %all-to-all-start.2 = ((f32[16,96,1]{1,2,0:T(1,128)}), f32[16,96,1]{1,2,0:T(1,128)S(1)}, u32[]{:S(2)}, u32[]{:S(2)}) async-start(f32[16,96,1]{1,2,0:T(1,128)} %bitcast.3), calls=%async_computation.2 | async-start | bytes 16384 | tf_op jit(solution)/shard_map/all_to_all | solution.py:59
Sparse Core Ops, SparseCore 0:
  60.9 10.4 all-gather.2
where the time goes:
time: 108 us; the launch traced here: 107 us
  blocking collectives  50.4 us (47%)
  between operations  14.2 us (13%)
  waiting for transfers between devices  13.1 us (12%)
  matrix products  8.99 us (8%)
  starting transfers between devices  7.48 us (7%)
  local copies, waits for them, and re-layouts  6.99 us (6%)
  other arithmetic  6.12 us (6%)
    all_to_all x1, blocking collectives, shards(): lax.all_to_all(outgoing, 'dp', split_axis=0, concat_axis=0, tiled=True)  46 us
    all_to_all x1, waiting for transfers between devices, shards(): lax.all_to_all(out_ids, 'dp', split_axis=0, concat_axis=0, tiled=True)  7.2 us
    all_to_all x1, waiting for transfers between devices, shards(): lax.all_to_all(best_all, 'dp', split_axis=0, concat_axis=0, tiled=True)  5.86 us
    dot_general x1, matrix products, shards(): lax.dot_general(queries, gathered, contract, preferred_element_type=jnp.f...  5.79 us
    gather x1, local copies, waits for them, and re-layouts, shards(): max_similarity = jnp.take(returned, slot)  4.46 us
    all_to_all x1, starting transfers between devices, shards(): lax.all_to_all(out_ids, 'dp', split_axis=0, concat_axis=0, tiled=True)  3.95 us
    all_to_all x1, starting transfers between devices, shards(): lax.all_to_all(best_all, 'dp', split_axis=0, concat_axis=0, tiled=True)  3.49 us
    psum x1, blocking collectives, shards(): squares = lax.psum(jnp.sum(embeddings * embeddings, axis=1), 'mp')  2.63 us
  transfers between devices with their start and end apart: 3, of which 2 were waited for; matrix products, arithmetic and copies ran while one was open for 4% of the time, Pallas kernels for 0%

commit v1 on v0

--- a/solution.py
+++ b/solution.py
@@ -6,16 +6,22 @@
 D = 1024
 
 
+def swap_cores(value):
+    size = lax.axis_size("mp")
+    return lax.ppermute(value, "mp", [(i, (i + 1) % size) for i in range(size)])
+
+
 def shards(embeddings, cluster_id, centroids, cluster_mass):
     owners = lax.axis_size("dp")
     row_count = embeddings.shape[0]
     slot_count = 2 * row_count
     capacity = slot_count // owners
     cluster_count = centroids.shape[0]
-    squares = lax.psum(jnp.sum(embeddings * embeddings, axis=1), "mp")
-    unit = (embeddings * lax.rsqrt(squares / D + 1e-06)[:, None]).astype(jnp.bfloat16)
     owner = cluster_id // cluster_count
     local = cluster_id - owner * cluster_count
+    partial = jnp.sum(embeddings * embeddings, axis=1)
+    squares = partial + swap_cores(partial)
+    unit = (embeddings * lax.rsqrt(squares / D + 1e-06)[:, None]).astype(jnp.bfloat16)
     owner_hot = (owner[:, None] == jnp.arange(owners, dtype=jnp.int32)[None, :]).astype(
         jnp.bfloat16
     )
@@ -26,24 +32,23 @@
     slot = owner * capacity + rank
     slot_index = jnp.arange(slot_count, dtype=jnp.int32)
     placed = slot_index[:, None] == slot[None, :]
+    out_ids = jnp.max(jnp.where(placed, local[None, :] + 1, 0), axis=1) - 1
     outgoing = jnp.dot(
         placed.astype(jnp.bfloat16), unit, preferred_element_type=jnp.float32
     ).astype(jnp.bfloat16)
-    out_ids = jnp.max(jnp.where(placed, local[None, :] + 1, 0), axis=1) - 1
-    incoming, in_ids = (
-        lax.all_to_all(outgoing, "dp", split_axis=0, concat_axis=0, tiled=True),
-        lax.all_to_all(out_ids, "dp", split_axis=0, concat_axis=0, tiled=True),
-    )
+    incoming = lax.all_to_all(outgoing, "dp", split_axis=0, concat_axis=0, tiled=True)
+    in_ids = lax.all_to_all(out_ids, "dp", split_axis=0, concat_axis=0, tiled=True)
+    other = swap_cores(incoming)
     member = (jnp.arange(cluster_count, dtype=jnp.int32)[:, None] == in_ids[None, :]).astype(
         jnp.bfloat16
     )
     sums = jnp.dot(member, incoming, preferred_element_type=jnp.float32)
     counts = jnp.sum(member.astype(jnp.float32), axis=1)
     new_centroids = (cluster_mass[:, None] * centroids + sums) / (cluster_mass + counts)[:, None]
-    half = slot_count // lax.axis_size("mp")
+    half = slot_count // 2
     start = lax.axis_index("mp") * half
     contract = (((1,), (1,)), ((), ()))
-    gathered = lax.all_gather(incoming, "mp", axis=1, tiled=True)
+    gathered = jnp.concatenate([incoming, other], axis=1)
     queries = lax.dynamic_slice_in_dim(gathered, start, half, 0)
     scores = lax.dot_general(queries, gathered, contract, preferred_element_type=jnp.float32)
     scores = scores / D
@@ -55,9 +60,11 @@
         & (query_pos[:, None] != slot_index[None, :])
     )
     best = jnp.max(jnp.where(same, scores, -1.0), axis=1)
-    best_all = lax.all_gather(best, "mp", axis=0, tiled=True)
+    partner = swap_cores(best)
+    first = lax.axis_index("mp") == 0
+    best_all = jnp.concatenate([jnp.where(first, best, partner), jnp.where(first, partner, best)])
     returned = lax.all_to_all(best_all, "dp", split_axis=0, concat_axis=0, tiled=True)
-    max_similarity = jnp.take(returned, slot)
+    max_similarity = jnp.max(jnp.where(placed, returned[:, None], -2.0), axis=0)
     return (max_similarity, new_centroids)
 
 

time: 108 us -> 83.9 us (0.78)
  between operations: 14.2 us -> 0.75 us
  local copies, waits for them, and re-layouts: 6.99 us -> 2 us
  blocking collectives: 50.4 us -> 45.9 us
  matrix products: 8.99 us -> 7.55 us
    gather x1 -> x0, local copies, waits for them, and re-layouts: 4.46 us -> none  [shards(): max_similarity = jnp.take(returned, slot)]
    psum x1 -> x0, blocking collectives: 2.63 us -> none  [shards(): squares = lax.psum(jnp.sum(embeddings * embeddings, axis=1), 'mp')]
    dot_general x1, matrix products: 5.79 us -> 3.32 us  [shards(): lax.dot_general(queries, gathered, contract, preferred_element_type=jnp.f...]
    all_gather x1 -> x0, blocking collectives: 1.82 us -> none  [shards(): best_all = lax.all_gather(best, 'mp', axis=0, tiled=True)]
    ppermute x0 -> x3, waiting for transfers between devices: none -> 1.34 us  [swap_cores(): return lax.ppermute(value, 'mp', [(i, (i + 1) % size) for i in range(size)])]
    select_n x2 -> x1, other arithmetic: 1.3 us -> 0.01 us  [shards(): jnp.where(first, best, partner)]
    reduce_max x0 -> x1, other arithmetic: none -> 1.19 us  [shards(): max_similarity = jnp.max(jnp.where(placed, returned[:, None], -2.0), axis=0)]
  transfers between devices with their start and end apart: 3 -> 5, of which waited for: 2 -> 4; matrix products, arithmetic and copies ran while one was open for 4% -> 7% of each run, Pallas kernels for 0% -> 0%
where the time goes in v1:
time: 83.9 us; the launch traced here: 83.5 us
  blocking collectives  45.9 us (55%)
  waiting for transfers between devices  13.4 us (16%)
  starting transfers between devices  8.07 us (10%)
  matrix products  7.55 us (9%)
  other arithmetic  5.91 us (7%)
  local copies, waits for them, and re-layouts  2 us (2%)
    all_to_all x1, blocking collectives, shards(): lax.all_to_all(outgoing, 'dp', split_axis=0, concat_axis=0, tiled=True)  45.9 us
    all_to_all x1, waiting for transfers between devices, shards(): lax.all_to_all(out_ids, 'dp', split_axis=0, concat_axis=0, tiled=True)  7.2 us
    all_to_all x1, waiting for transfers between devices, shards(): lax.all_to_all(best_all, 'dp', split_axis=0, concat_axis=0, tiled=True)  4.84 us
    all_to_all x1, starting transfers between devices, shards(): lax.all_to_all(out_ids, 'dp', split_axis=0, concat_axis=0, tiled=True)  3.95 us
    all_to_all x1, starting transfers between devices, shards(): lax.all_to_all(best_all, 'dp', split_axis=0, concat_axis=0, tiled=True)  3.49 us
    dot_general x1, matrix products, shards(): lax.dot_general(queries, gathered, contract, preferred_element_type=jnp.f...  3.32 us
    dot_general x1, matrix products, shards(): sums = jnp.dot(member, incoming, preferred_element_type=jnp.float32)  2.42 us
    reduce_sum x1, other arithmetic, shards(): partial = jnp.sum(embeddings * embeddings, axis=1)  1.71 us
  transfers between devices with their start and end apart: 5, of which 4 were waited for; matrix products, arithmetic and copies ran while one was open for 7% of the time, Pallas kernels for 0%

profile of v1, /device:TPU:0, one launch (start us, length us, event | category | flops | bytes accessed | tf_op | source)
XLA Modules:
  0.0 83.5 jit_solution(9438694538765811415)
XLA Ops:
  0.6 0.0 copy-start
  0.6 0.0 copy-start.1
  0.6 1.7 %multiply_reduce_fusion = f32[768]{0:T(1024)S(1)} fusion(f32[768,512]{1,0:T(8,128)} %param.4), kind=kLoop, calls=%fused_computation.20 | loop fusion | flops 785664 | bytes 1575936 | tf_op jit(solution)/shard_map/reduce_sum | solution.py:22
  2.4 0.6 collective-permute-start
  2.9 0.0 copy-done.1
  2.9 0.3 fusion.12
  3.3 0.4 collective-permute-done
  3.8 0.0 copy-done
  3.8 1.5 %fusion.2 = bf16[1536,512]{1,0:T(8,128)(2,1)S(1)} fusion(s32[768]{0:T(1024)S(1)} %get-tuple-element.7, f32[768,512]{1,0:T(8,128)S(1)} %copy-done, f32[768]{0:T(1024)S(1)} %add_rsqrt_fusion), kind=kOutput, calls=%fused_computation.10 | convolution fusion | flops 1210712064 | bytes 3151872 | tf_op jit(solution)/shard_map/dot_general | solution.py:36
  5.2 45.9 %all_to_all.27 = bf16[16,96,512]{2,1,0:T(8,128)(2,1)S(1)} all-to-all(bf16[16,96,512]{2,1,0:T(8,128)(2,1)S(1)} %bitcast.10), channel_id=1, replica_groups=mesh['dp'=16,'mp'=2] {'dp'}, dimensions={0} | all-to-all | bytes 3145728 | tf_op jit(solution)/shard_map/all_to_all | solution.py:39
  51.1 0.0 collective-permute-start.1
  51.1 0.7 select_reduce_fusion.2
  51.8 0.7 sub.23
  52.5 3.9 %all-to-all-start = ((s32[16,96,1]{1,2,0:T(1,128)}), s32[16,96,1]{1,2,0:T(1,128)S(1)}, u32[]{:S(2)}, u32[]{:S(2)}) async-start(s32[16,96,1]{1,2,0:T(1,128)} %bitcast), calls=%async_computation | async-start | bytes 16384 | tf_op jit(solution)/shard_map/all_to_all | solution.py:40
  56.5 7.2 %all-to-all-done = s32[16,96,1]{1,2,0:T(1,128)S(1)} async-done(((s32[16,96,1]{1,2,0:T(1,128)}), s32[16,96,1]{1,2,0:T(1,128)S(1)}, u32[]{:S(2)}, u32[]{:S(2)}) %all-to-all-start) | async-done | bytes 6176 | tf_op jit(solution)/shard_map/all_to_all | solution.py:40
  63.7 0.5 broadcast.60
  64.2 0.7 reduce.6
  64.9 0.1 all_to_all.19
  64.9 0.1 broadcast_compare_fusion
  65.0 0.0 collective-permute-done.1
  65.0 0.0 copy-start.2
  65.0 3.3 %select_reduce_fusion.1 = f32[768]{0:T(1024)S(1)} fusion(bf16[1536,512]{1,0:T(8,128)(2,1)S(1)} %collective-permute-done.1, bf16[1536,512]{1,0:T(8,128)(2,1)S(1)} %bitcast.8, s32[768]{0:T(1024)S(1)} %iota_add_fusion, s32[1536]{0:T(1024)S(1)} %all_to_all.19, s32[768]{0:T(1024)S(1)} %get-tuple-element.3, pred[768]{0:T(1024)(128)(4,1)S(1)} %get-tuple-element.2, ...), kind=kOutput, calls=%fused_computation.1 | convolution fusion | flops 2433613056 | bytes 6311940 | tf_op jit(solution)/shard_map/dot_general | solution.py:53
  68.3 0.1 collective-permute-start.2
  68.4 0.2 convert_reduce_fusion
  68.7 0.0 copy-done.2
  68.7 0.9 %collective-permute-done.2 = f32[768]{0:T(1024)S(1)} collective-permute-done((f32[768]{0:T(1024)S(1)}, f32[768]{0:T(1024)S(1)}, u32[]{:S(2)}, u32[]{:S(2)}) %collective-permute-start.2) | collective-permute-done | bytes 3104 | tf_op jit(solution)/shard_map/ppermute | solution.py:11
  69.6 0.1 concatenate.12
  69.7 0.1 concatenate.13
  69.7 0.6 pad_maximum_fusion.2
  70.3 3.5 %all-to-all-start.2 = ((f32[16,96,1]{1,2,0:T(1,128)}), f32[16,96,1]{1,2,0:T(1,128)S(1)}, u32[]{:S(2)}, u32[]{:S(2)}) async-start(f32[16,96,1]{1,2,0:T(1,128)} %bitcast.3), calls=%async_computation.2 | async-start | bytes 16384 | tf_op jit(solution)/shard_map/all_to_all | solution.py:66
  73.8 2.4 %fusion.10 = f32[256,512]{1,0:T(8,128)} fusion(bf16[1536,512]{1,0:T(8,128)(2,1)S(1)} %bitcast.9, s32[1536]{0:T(1024)S(1)} %all_to_all.19, f32[256,512]{1,0:T(8,128)} %param.6, f32[256]{0:T(256)S(1)} %add.57, f32[256]{0:T(256)S(1)} %copy-done.2), kind=kOutput, calls=%fused_computation.22 | convolution fusion | flops 403439616 | bytes 2629632 | tf_op jit(solution)/shard_map/dot_general | solution.py:45
  76.3 4.8 %all-to-all-done.2 = f32[16,96,1]{1,2,0:T(1,128)S(1)} async-done(((f32[16,96,1]{1,2,0:T(1,128)}), f32[16,96,1]{1,2,0:T(1,128)S(1)}, u32[]{:S(2)}, u32[]{:S(2)}) %all-to-all-start.2) | async-done | bytes 6176 | tf_op jit(solution)/shard_map/all_to_all | solution.py:66
  81.1 0.5 broadcast.61
  81.6 0.7 reduce.7
  82.3 0.1 broadcast_in_dim.29
  82.4 1.2 %select_reduce_fusion = f32[768]{0:T(1024)} fusion(f32[1536]{0:T(1024)S(1)} %broadcast_in_dim.29, s32[768]{0:T(1024)S(1)} %get-tuple-element.7), kind=kLoop, calls=%fused_computation | loop fusion | flops 3538176 | bytes 12288 | tf_op jit(solution)/shard_map/reduce_max | solution.py:67
  (7 shorter events, 0.0 us)
Async XLA Ops:
  0.6 3.1 %copy-start = (f32[768,512]{1,0:T(8,128)S(1)}, f32[768,512]{1,0:T(8,128)}, u32[]{:S(2)}) copy-start(f32[768,512]{1,0:T(8,128)} %param.4) | copy-start | bytes 4718596
  0.6 2.3 %copy-start.1 = (s32[768]{0:T(1024)S(1)}, s32[768]{0:T(1024)}, u32[]{:S(2)}) copy-start(s32[768]{0:T(1024)} %param.5) | copy-start | bytes 9220
  2.4 1.4 %collective-permute-start = (f32[768]{0:T(1024)S(1)}, f32[768]{0:T(1024)S(1)}, u32[]{:S(2)}, u32[]{:S(2)}) collective-permute-start(f32[768]{0:T(1024)S(1)} %multiply_reduce_fusion), channel_id=1, source_target_pairs={{0,1},{1,0},{2,3},{3,2},{4,5},{5,4},{6,7},{7,6},{8,9},{9,8},{10,11... | collective-permute-start | bytes 9224 | tf_op jit(solution)/shard_map/ppermute | solution.py:11
  51.1 13.9 %collective-permute-start.1 = (bf16[1536,512]{1,0:T(8,128)(2,1)S(1)}, bf16[1536,512]{1,0:T(8,128)(2,1)S(1)}, u32[]{:S(2)}, u32[]{:S(2)}) collective-permute-start(bf16[1536,512]{1,0:T(8,128)(2,1)S(1)} %bitcast.7), channel_id=1, source_target_pairs={{0,1},{1,0},{2,3},{3,2},{4,5},{5,4},{6,7},{7,6},{8,9},{9,8},{10,11... | collective-permute-start | bytes 4718600 | tf_op jit(solution)/shard_map/ppermute | solution.py:11
  52.5 11.2 %all-to-all-start = ((s32[16,96,1]{1,2,0:T(1,128)}), s32[16,96,1]{1,2,0:T(1,128)S(1)}, u32[]{:S(2)}, u32[]{:S(2)}) async-start(s32[16,96,1]{1,2,0:T(1,128)} %bitcast), calls=%async_computation | async-start | bytes 16384 | tf_op jit(solution)/shard_map/all_to_all | solution.py:40
  65.0 3.6 %copy-start.2 = (f32[256]{0:T(256)S(1)}, f32[256]{0:T(256)}, u32[]{:S(2)}) copy-start(f32[256]{0:T(256)} %param.7) | copy-start | bytes 3076
  68.3 1.2 %collective-permute-start.2 = (f32[768]{0:T(1024)S(1)}, f32[768]{0:T(1024)S(1)}, u32[]{:S(2)}, u32[]{:S(2)}) collective-permute-start(f32[768]{0:T(1024)S(1)} %select_reduce_fusion.1), channel_id=1, source_target_pairs={{0,1},{1,0},{2,3},{3,2},{4,5},{5,4},{6,7},{7,6},{8,9},{9,8},{10,11... | collective-permute-start | bytes 9224 | tf_op jit(solution)/shard_map/ppermute | solution.py:11
  70.3 10.8 %all-to-all-start.2 = ((f32[16,96,1]{1,2,0:T(1,128)}), f32[16,96,1]{1,2,0:T(1,128)S(1)}, u32[]{:S(2)}, u32[]{:S(2)}) async-start(f32[16,96,1]{1,2,0:T(1,128)} %bitcast.3), calls=%async_computation.2 | async-start | bytes 16384 | tf_op jit(solution)/shard_map/all_to_all | solution.py:66
